TPU v7x, 32 devices: a 4x4x1 block of a 4x4x8 slice. The times are simulated.
32 devices in a mesh: dp: 1 (over z), stage: 32 (over y, x, core).
Axes of the slice: x: 4, y: 4, z: 1, core: 2. Of those that a mesh axis runs over, the one named last changes fastest.
The devices are a block of a 4x4x8 slice.
Arguments:
- x_in: bfloat16 [64, 64, 256], P('dp')
- y_target: bfloat16 [64, 64, 256], P('dp')
- w_up: bfloat16 [32, 256, 1024], P('stage')
- w_down: bfloat16 [32, 1024, 256], P('stage')
- norm_gain: float32 [32, 256], P('stage')
Outputs:
- output 1: float32 [32, 256, 1024], P(('dp', 'stage'))
- output 2: float32 [32, 1024, 256], P(('dp', 'stage'))
- output 3: float32 [32, 256], P(('dp', 'stage'))
- output 4: float32 [1], P('dp')
All inputs are finite; a program needn't handle non-finite values.
Results may differ from a plain program's by a relative error of at most 0.00668016.
Values are sent between devices in bfloat16 or wider.
A program may use at most 768 MiB of HBM per device.

v0:
```python
import jax
import jax.numpy as jnp
from jax import lax
from jax.sharding import PartitionSpec as P

NORM_EPS = 1e-6


def rms_norm(x_act, gain_row):
    x_float = x_act.astype(jnp.float32)
    inv_rms = lax.rsqrt(jnp.mean(x_float * x_float, axis=-1, keepdims=True) + NORM_EPS)
    return x_float * inv_rms * gain_row


def gelu_tanh(hidden):
    return jax.nn.gelu(hidden, approximate=True)


def layer_forward(x_act, w_up_l, w_down_l, gain_l):
    normed = rms_norm(x_act, gain_l[:, None, :]).astype(jnp.bfloat16)
    hidden = jnp.einsum('zbd,zdf->zbf', normed, w_up_l, preferred_element_type=jnp.float32)
    gelu_out = gelu_tanh(hidden).astype(jnp.bfloat16)
    mlp_out = jnp.einsum('zbf,zfd->zbd', gelu_out, w_down_l, preferred_element_type=jnp.float32)
    return (x_act.astype(jnp.float32) + mlp_out).astype(jnp.bfloat16)


def layer_backward(x_act, grad_out, w_up_l, w_down_l, gain_l):
    normed_f, norm_vjp = jax.vjp(rms_norm, x_act.astype(jnp.float32), gain_l[:, None, :])
    normed = normed_f.astype(jnp.bfloat16)
    hidden = jnp.einsum('zbd,zdf->zbf', normed, w_up_l, preferred_element_type=jnp.float32)
    gelu_f, gelu_vjp = jax.vjp(gelu_tanh, hidden)
    gelu_out = gelu_f.astype(jnp.bfloat16)
    grad_gelu = jnp.einsum('zbd,zfd->zbf', grad_out, w_down_l, preferred_element_type=jnp.float32)
    grad_hidden = gelu_vjp(grad_gelu.astype(jnp.bfloat16).astype(jnp.float32))[0].astype(jnp.bfloat16)
    grad_normed = jnp.einsum('zbf,zdf->zbd', grad_hidden, w_up_l, preferred_element_type=jnp.float32)
    grad_x, grad_gain = norm_vjp(grad_normed.astype(jnp.bfloat16).astype(jnp.float32))
    grad_in = (grad_out.astype(jnp.float32) + grad_x).astype(jnp.bfloat16)
    grad_w_down = jnp.einsum('zbf,zbd->zfd', gelu_out, grad_out, preferred_element_type=jnp.float32)
    grad_w_up = jnp.einsum('zbd,zbf->zdf', normed, grad_hidden, preferred_element_type=jnp.float32)
    return grad_in, grad_w_up, grad_w_down, grad_gain[:, 0, :]


def solution(mesh):
    n_stages = mesh.shape['stage']
    next_perm = [(src_dev, src_dev + 1) for src_dev in range(n_stages - 1)]
    prev_perm = [(src_dev + 1, src_dev) for src_dev in range(n_stages - 1)]
    mirror_perm = [(src_dev, n_stages - 1 - src_dev) for src_dev in range(n_stages)]

    def stage_body(x_in, y_target, w_up, w_down, norm_gain):
        n_micro, n_tok, d_model = x_in.shape
        n_layers = w_up.shape[0]
        d_ff = w_up.shape[2]
        half_micro = n_micro // 2
        n_ticks = half_micro + n_stages - 1
        loss_scale = 1.0 / (n_micro * n_tok * d_model)
        stage_idx = lax.axis_index('stage')
        fwd_depth = jnp.stack([stage_idx, n_stages - 1 - stage_idx])
        back_depth = n_stages - 1 - fwd_depth
        micro_base = jnp.array([0, 1], jnp.int32) * half_micro
        is_first = (fwd_depth == 0)[:, None, None]
        is_last = fwd_depth == n_stages - 1

        w_up_both = jnp.stack([w_up, lax.ppermute(w_up, 'stage', mirror_perm)], axis=1)
        w_down_both = jnp.stack([w_down, lax.ppermute(w_down, 'stage', mirror_perm)], axis=1)
        gain_both = jnp.stack([norm_gain, lax.ppermute(norm_gain, 'stage', mirror_perm)], axis=1)

        def pick_rows(source, row_idx):
            return jnp.stack([lax.dynamic_index_in_dim(source, row_idx[dir_idx], 0, keepdims=False) for dir_idx in range(2)])

        def pick_pairs(source, row_idx):
            return jnp.stack([lax.dynamic_index_in_dim(source[dir_idx], row_idx[dir_idx], 0, keepdims=False) for dir_idx in range(2)])

        def fwd_tick(tick_idx, loop_state):
            recv_act, saved_inputs, top_grads, loss_sum = loop_state
            micro_idx = tick_idx - fwd_depth
            is_valid = (micro_idx >= 0) & (micro_idx < half_micro)
            micro_clip = jnp.clip(micro_idx, 0, half_micro - 1)
            layer_act = jnp.where(is_first, pick_rows(x_in, micro_clip + micro_base), recv_act)
            layer_inputs = []
            for layer_idx in range(n_layers):
                layer_inputs.append(layer_act)
                layer_act = layer_forward(layer_act, w_up_both[layer_idx], w_down_both[layer_idx], gain_both[layer_idx])
            stacked_inputs = jnp.stack(layer_inputs, axis=1)
            slot_idx = jnp.where(is_valid, micro_clip, half_micro)
            for dir_idx in range(2):
                saved_inputs = lax.dynamic_update_slice(saved_inputs, stacked_inputs[dir_idx][None, None], (dir_idx, slot_idx[dir_idx], 0, 0, 0))
            target_act = pick_rows(y_target, micro_clip + micro_base)
            error_val = layer_act.astype(jnp.float32) - target_act.astype(jnp.float32)
            at_top = is_valid & is_last
            loss_sum = loss_sum + jnp.sum(jnp.where(at_top[:, None, None], error_val * error_val, 0.0))
            top_val = (2.0 * loss_scale * error_val).astype(jnp.bfloat16)
            top_slot = jnp.where(at_top, micro_clip, half_micro)
            for dir_idx in range(2):
                top_grads = lax.dynamic_update_slice(top_grads, top_val[dir_idx][None, None], (dir_idx, top_slot[dir_idx], 0, 0))
            recv_act = jnp.stack([lax.ppermute(layer_act[0], 'stage', next_perm), lax.ppermute(layer_act[1], 'stage', prev_perm)])
            return recv_act, saved_inputs, top_grads, loss_sum

        fwd_init = (jnp.zeros((2, n_tok, d_model), jnp.bfloat16),
                    jnp.zeros((2, half_micro + 1, n_layers, n_tok, d_model), jnp.bfloat16),
                    jnp.zeros((2, half_micro + 1, n_tok, d_model), jnp.bfloat16),
                    jnp.zeros((), jnp.float32))
        fwd_out = lax.fori_loop(0, n_ticks, fwd_tick, fwd_init)
        saved_inputs = fwd_out[1]
        top_grads = fwd_out[2]
        loss_sum = fwd_out[3]

        def bwd_tick(tick_idx, loop_state):
            recv_grad, acc_up, acc_down, acc_gain = loop_state
            micro_idx = tick_idx - back_depth
            is_valid = (micro_idx >= 0) & (micro_idx < half_micro)
            micro_clip = jnp.clip(micro_idx, 0, half_micro - 1)
            grad_act = jnp.where(is_last[:, None, None], pick_pairs(top_grads, micro_clip), recv_grad)
            grad_act = jnp.where(is_valid[:, None, None], grad_act, jnp.zeros_like(grad_act))
            layer_inputs = pick_pairs(saved_inputs, micro_clip)
            new_up = list(acc_up)
            new_down = list(acc_down)
            new_gain = list(acc_gain)
            for layer_idx in reversed(range(n_layers)):
                grad_act, grad_up_l, grad_down_l, grad_gain_l = layer_backward(layer_inputs[:, layer_idx], grad_act, w_up_both[layer_idx], w_down_both[layer_idx], gain_both[layer_idx])
                new_up[layer_idx] = new_up[layer_idx] + grad_up_l
                new_down[layer_idx] = new_down[layer_idx] + grad_down_l
                new_gain[layer_idx] = new_gain[layer_idx] + grad_gain_l
            recv_grad = jnp.stack([lax.ppermute(grad_act[0], 'stage', prev_perm), lax.ppermute(grad_act[1], 'stage', next_perm)])
            return recv_grad, tuple(new_up), tuple(new_down), tuple(new_gain)

        bwd_init = (jnp.zeros((2, n_tok, d_model), jnp.bfloat16),
                    tuple(jnp.zeros((2, d_model, d_ff), jnp.float32) for layer_idx in range(n_layers)),
                    tuple(jnp.zeros((2, d_ff, d_model), jnp.float32) for layer_idx in range(n_layers)),
                    tuple(jnp.zeros((2, d_model), jnp.float32) for layer_idx in range(n_layers)))
        bwd_out = lax.fori_loop(0, n_ticks, bwd_tick, bwd_init)

        def join_pair(acc_list):
            own_part = jnp.stack([acc_list[layer_idx][0] for layer_idx in range(n_layers)])
            other_part = jnp.stack([acc_list[layer_idx][1] for layer_idx in range(n_layers)])
            return own_part + lax.ppermute(other_part, 'stage', mirror_perm)

        dw_up = join_pair(bwd_out[1])
        dw_down = join_pair(bwd_out[2])
        dgain = join_pair(bwd_out[3])
        loss_total = lax.psum(loss_sum, 'stage') * loss_scale
        return dw_up, dw_down, dgain, loss_total.reshape(1)

    return jax.shard_map(stage_body, mesh=mesh,
                         in_specs=(P('dp'), P('dp'), P('stage'), P('stage'), P('stage')),
                         out_specs=(P(('dp', 'stage')), P(('dp', 'stage')), P(('dp', 'stage')), P('dp')),
                         check_vma=False)
```

profile of v0, /device:TPU:97, one launch (start us, length us, event | category | flops | bytes accessed | tf_op | source)
XLA Modules:
  0.0 3497.9 jit_solution(17611850979444984677)
XLA Ops:
  0.6 8.4 collective-permute-start.5
  14.3 18.0 collective-permute-done.4
  37.0 1587.6 %while.42 = (s32[]{:T(128)}, bf16[2,64,256]{2,1,0:T(8,128)(2,1)S(1)}, bf16[2,33,1,64,256]{4,3,2,1,0:T(8,128)(2,1)S(1)}, bf16[2,33,64,256]{3,2,1,0:T(8,128)(2,1)}...) while((s32[]{:T(128)}, ...), condition=%wide.region_3.4_spmd.clone, body=%wide.region_0.3_spmd.clone.sunk | while | flops 136183968 | bytes 3609163 | solution.py:102
  282.0 5.8 collective-permute-start.1
  307.5 5.8 collective-permute-start.1
  333.0 5.8 collective-permute-start.1
  358.5 5.8 collective-permute-start.1
  384.0 5.8 collective-permute-start.1
  409.6 5.8 collective-permute-start.1
  435.1 5.8 collective-permute-start.1
  460.6 5.8 collective-permute-start.1
  486.1 5.8 collective-permute-start.1
  511.6 5.8 collective-permute-start.1
  537.1 5.8 collective-permute-start.1
  562.7 5.8 collective-permute-start.1
  588.2 5.8 collective-permute-start.1
  639.2 5.8 collective-permute-start.1
  690.2 5.8 collective-permute-start.1
  741.3 5.8 collective-permute-start.1
  766.8 5.8 collective-permute-start.1
  1625.3 1755.9 %while.43 = (s32[]{:T(128)}, bf16[2,64,256]{2,1,0:T(8,128)(2,1)}, f32[2,256,1024]{2,1,0:T(8,128)}, f32[2,1024,256]{2,1,0:T(8,128)}, f32[2,256]{1,0:T(2,128)}, /*...) while((s32[]{:T(128)}, bf16[2,64,256]{2,1,0:T(8,128)(2,1)}, ...), condition=%wide.region_8.9_spmd.clone, body=%wide.region_4.8_spmd.clone.sunk | while | flops 343147776 | bytes 33856364 | solution.py:130
  1690.3 6.7 collective-permute-start.2
  1746.3 6.7 collective-permute-start.2
  3395.2 96.6 %psum.7 = f32[]{:T(128)} all-reduce(f32[]{:T(128)} %get-tuple-element.528), channel_id=1, replica_groups=mesh['dp'=1,'stage'=32] {'stage'}, use_global_device_ids=true, to_apply=%region_9.10 | all-reduce | flops 1 | bytes 8 | tf_op jit(solution)/shard_map/psum | solution.py:140
  (4489 shorter events, 2250.3 us)
Async XLA Ops:
  0.6 32.3 collective-permute-start.5
  9.0 25.0 collective-permute-start.6
  9.2 23.1 collective-permute-start.4
  280.0 17.8 collective-permute-start
  331.1 17.8 collective-permute-start
  382.1 17.8 collective-permute-start
  433.1 17.8 collective-permute-start
  484.2 17.8 collective-permute-start
  535.2 17.8 collective-permute-start
  662.8 17.8 collective-permute-start
  713.8 17.8 collective-permute-start
  764.8 17.8 collective-permute-start
  815.9 17.8 collective-permute-start
  866.9 17.8 collective-permute-start
  917.9 17.8 collective-permute-start
  969.0 17.8 collective-permute-start
  1020.0 17.8 collective-permute-start
  1147.6 17.8 collective-permute-start
  1198.6 17.8 collective-permute-start
  1249.6 17.8 collective-permute-start
  1300.7 17.8 collective-permute-start
  3383.6 109.4 %collective-permute-start.8 = (f32[1,1024,256]{2,1,0:T(8,128)}, f32[1,1024,256]{2,1,0:T(8,128)}, u32[]{:S(2)}, u32[]{:S(2)}) collective-permute-start(f32[1,1024,256]{2,1,0:T(8,128)} %slice.191), channel_id=1, source_target_pairs={{0,31},{1,30},{2,29},{3,28},{4,27},{5,26},{6,25},{7,24},{8,23},{9,... | collective-permute-start | bytes 3145736 | tf_op jit(solution)/shard_map/ppermute | solution.py:135
  3390.1 105.6 %collective-permute-start.7 = (f32[1,256,1024]{2,1,0:T(8,128)}, f32[1,256,1024]{2,1,0:T(8,128)S(1)}, u32[]{:S(2)}, u32[]{:S(2)}) collective-permute-start(f32[1,256,1024]{2,1,0:T(8,128)} %slice.189), channel_id=1, source_target_pairs={{0,31},{1,30},{2,29},{3,28},{4,27},{5,26},{6,25},{7,24},{8,23},{9,... | collective-permute-start | bytes 3145736 | tf_op jit(solution)/shard_map/ppermute | solution.py:135
  3390.1 102.3 %collective-permute-start.9 = (f32[1,256]{1,0:T(1,128)S(1)}, f32[1,256]{1,0:T(1,128)S(1)}, u32[]{:S(2)}, u32[]{:S(2)}) collective-permute-start(f32[1,256]{1,0:T(1,128)S(1)} %slice.193), channel_id=1, source_target_pairs={{0,31},{1,30},{2,29},{3,28},{4,27},{5,26},{6,25},{7,24},{8,23},{9,... | collective-permute-start | bytes 3080 | tf_op jit(solution)/shard_map/ppermute | solution.py:135
  (1182 other events, 6261.9 us)
where the time goes:
time: 3540 us; the launch traced here: 3500 us
  loops' own time  1010 us (29%)
  starting transfers between devices  972 us (27%)
  matrix products  681 us (19%)
  local copies, waits for them, and re-layouts  554 us (16%)
  other arithmetic  162 us (5%)
  blocking collectives  96.6 us (3%)
    another operation x1, loops' own time, stage_body(): fwd_out = lax.fori_loop(0, n_ticks, fwd_tick, fwd_init)  748 us
    ppermute x63, starting transfers between devices, bwd_tick(): lax.ppermute(grad_act[1], 'stage', next_perm)  358 us
    ppermute x63, starting transfers between devices, fwd_tick(): lax.ppermute(layer_act[0], 'stage', next_perm)  344 us
    another operation x1, loops' own time, stage_body(): bwd_out = lax.fori_loop(0, n_ticks, bwd_tick, bwd_init)  263 us
    dot_general x63, matrix products, layer_backward(): jnp.einsum('zbd,zbf->zdf', normed, grad_hidden, preferred_element_type=jn...  219 us
    dot_general x63, matrix products, layer_backward(): jnp.einsum('zbf,zbd->zfd', gelu_out, grad_out, preferred_element_type=jnp...  217 us
    slice x126, local copies, waits for them, and re-layouts, pick_pairs(): source[dir_idx]  211 us
    dot_general x63, matrix products, layer_forward(): jnp.einsum('zbf,zfd->zbd', gelu_out, w_down_l, preferred_element_type=jnp...  153 us

commit v1 on v0

v1 whole, which is shorter than its diff:
```python
import functools

import jax
import jax.numpy as jnp
from jax import lax
from jax.experimental import pallas as pl
from jax.experimental.pallas import tpu as pltpu
from jax.sharding import PartitionSpec as P

NORM_EPS = 1e-6
SEG = 8
N_CHUNKS = 4
GELU_C = 0.7978845608028654
GELU_A = 0.044715
MESH = pl.DeviceIdType.MESH
F32 = jnp.float32
BF16 = jnp.bfloat16


def dot_nn(lhs, rhs):
    return lax.dot_general(lhs, rhs, (((1,), (0,)), ((), ())), preferred_element_type=F32)


def dot_nt(lhs, rhs):
    return lax.dot_general(lhs, rhs, (((1,), (1,)), ((), ())), preferred_element_type=F32)


def dot_tn(lhs, rhs):
    return lax.dot_general(lhs, rhs, (((0,), (0,)), ((), ())), preferred_element_type=F32)


def gelu_parts(hidden):
    sq = hidden * hidden
    tanh_val = jnp.tanh(hidden * (GELU_C + (GELU_C * GELU_A) * sq))
    half = 0.5 * hidden
    value = half + half * tanh_val
    slope = (0.5 + 0.5 * tanh_val) + (half * (1.0 - tanh_val * tanh_val)) * (GELU_C + (3.0 * GELU_C * GELU_A) * sq)
    return value, slope


def inv_rms_of(x_float):
    return lax.rsqrt(jnp.mean(x_float * x_float, axis=-1, keepdims=True) + NORM_EPS)


def fold_rows(block):
    rows, cols = block.shape
    return jnp.sum(block.reshape(rows // 8, 8, cols), axis=0)


def step_kernel(n_stages, loss_scale,
                x_hbm, y_hbm, wu_hbm, wd_hbm, gain_ref,
                dwu_ref, dwd_ref, dgain_ref, loss_ref,
                wu, wd, gains, acts, grads, slopes, act_stash, grad_stash, targets, dwd_t,
                dg_part, dg_stash, loss_part, loss_stash, loss_total,
                load_sem, x_sem, y_sem, agu_send, agu_recv, agd_send, agd_recv, gain_send, gain_recv,
                as_send, as_recv, gs_send, gs_recv, fwd_send, fwd_recv, bwd_send, bwd_recv,
                dg_send, dg_recv, lrow_send, lrow_recv, lcol_send, lcol_recv):
    n_rows = n_stages // SEG
    n_chips = SEG // 2
    chunk = acts.shape[2]
    d_model = acts.shape[3]
    d_ff = wu.shape[2]
    me = lax.axis_index('stage')
    row = lax.div(me, SEG)
    r = lax.rem(me, SEG)
    chip = lax.div(r, 2)
    core = lax.rem(r, 2)
    row_base = row * SEG
    left = lax.rem(chip + n_chips - 1, n_chips) * 2 + core
    right = lax.rem(chip + 1, n_chips) * 2 + core
    across = lax.rem(chip + 2, n_chips) * 2 + core
    flip = 1 - 2 * core
    sib = r + flip

    def rcopy(src, dst, send_sem, recv_sem, dev):
        return pltpu.make_async_remote_copy(src_ref=src, dst_ref=dst, send_sem=send_sem, recv_sem=recv_sem,
                                            device_id={'stage': dev}, device_id_type=MESH)

    load_u = pltpu.make_async_copy(wu_hbm.at[0], wu.at[r], load_sem.at[0])
    load_d = pltpu.make_async_copy(wd_hbm.at[0], wd.at[r], load_sem.at[1])
    load_u.start()
    load_d.start()

    def x_load(k):
        first = pl.multiple_of((r * N_CHUNKS + k) * chunk, chunk)
        return pltpu.make_async_copy(x_hbm.at[pl.ds(first, chunk)], acts.at[0, k], x_sem.at[k])

    def y_load(k):
        first = pl.multiple_of((r * N_CHUNKS + k) * chunk, chunk)
        return pltpu.make_async_copy(y_hbm.at[pl.ds(first, chunk)], targets.at[k], y_sem.at[k])

    @pl.when(row == 0)
    def _():
        for k in range(N_CHUNKS):
            x_load(k).start()

    @pl.when(row == n_rows - 1)
    def _():
        for k in range(N_CHUNKS):
            y_load(k).start()

    gains[r] = jnp.broadcast_to(gain_ref[...], (8, d_model))
    dg_part[...] = jnp.zeros_like(dg_part)
    loss_part[...] = jnp.zeros_like(loss_part)

    barrier = pltpu.get_barrier_semaphore()
    for step in range(1, SEG):
        pl.semaphore_signal(barrier, inc=1, device_id={'stage': row_base + lax.rem(r + step, SEG)}, device_id_type=MESH)
    for step in range(1, n_rows):
        pl.semaphore_signal(barrier, inc=1, device_id={'stage': lax.rem(row + step, n_rows) * SEG + r}, device_id_type=MESH)
    pl.semaphore_wait(barrier, SEG - 1 + n_rows - 1)

    def u_copy(slot, dev):
        return rcopy(wu.at[slot], wu.at[slot], agu_send, agu_recv.at[slot], row_base + dev)

    def d_copy(slot, dev):
        return rcopy(wd.at[slot], wd.at[slot], agd_send, agd_recv.at[slot], row_base + dev)

    load_u.wait()
    load_d.wait()
    u_copy(r, right).start()
    d_copy(r, left).start()
    d_copy(r, right).start()
    u_copy(r, left).start()
    u_copy(r, sib).start()
    d_copy(r, sib).start()
    for step in range(1, SEG):
        rcopy(gains.at[r], gains.at[r], gain_send, gain_recv, row_base + lax.rem(r + step, SEG)).start()

    u_copy(left, r).wait_recv()
    u_copy(left, right).start()
    u_copy(left, sib).start()
    d_copy(right, r).wait_recv()
    d_copy(right, left).start()
    d_copy(right, sib).start()
    d_copy(left, r).wait_recv()
    d_copy(left, sib).start()
    u_copy(right, r).wait_recv()
    u_copy(right, sib).start()
    u_copy(across, r).wait_recv()
    u_copy(across, sib).start()
    d_copy(across, r).wait_recv()
    d_copy(across, sib).start()
    for slot in (sib, left + flip, right + flip, across + flip):
        u_copy(slot, r).wait_recv()
        d_copy(slot, r).wait_recv()
    rcopy(gains.at[pl.ds(0, SEG - 1)], gains.at[pl.ds(0, SEG - 1)], gain_send, gain_recv, me).wait_recv()

    def act_ship(layer, k):
        return rcopy(acts.at[layer, k], act_stash.at[r, k], as_send, as_recv, row_base + layer)

    def grad_ship(layer, k):
        return rcopy(grads.at[layer + 1, k], grad_stash.at[r, k], gs_send, gs_recv, row_base + layer)

    def fwd_layer(layer, k):
        x_float = acts[layer, k].astype(F32)
        normed = (x_float * inv_rms_of(x_float) * gains[layer, 0:1, :]).astype(BF16)
        hidden = dot_nn(normed, wu[layer])
        value, slope = gelu_parts(hidden)
        slopes[layer, k] = slope
        out = x_float + dot_nn(value.astype(BF16), wd[layer])
        acts[layer + 1, k] = out.astype(BF16)

        @pl.when(layer != r)
        def _():
            act_ship(layer, k).start()
        return k

    def fwd_chunk(k, carry):
        @pl.when(row == 0)
        def _():
            x_load(k).wait()

        @pl.when(row > 0)
        def _():
            rcopy(acts.at[0, k], acts.at[0, k], fwd_send, fwd_recv.at[k], me).wait_recv()

        lax.fori_loop(0, SEG, fwd_layer, k)

        @pl.when(row < n_rows - 1)
        def _():
            rcopy(acts.at[SEG, k], acts.at[0, k], fwd_send, fwd_recv.at[k], me + SEG).start()

        @pl.when(row == n_rows - 1)
        def _():
            y_load(k).wait()
            error_val = acts[SEG, k].astype(F32) - targets[k].astype(F32)
            loss_part[...] += fold_rows(error_val * error_val)
            grads[SEG, k] = ((2.0 * loss_scale) * error_val).astype(BF16)
        return carry

    lax.fori_loop(0, N_CHUNKS, fwd_chunk, 0)

    @pl.when(row == n_rows - 1)
    def _():
        loss_stash[r] = loss_part[...]
        for step in range(1, SEG):
            rcopy(loss_stash.at[r], loss_stash.at[r], lrow_send, lrow_recv, row_base + lax.rem(r + step, SEG)).start()

    def bwd_layer(step, k):
        layer = SEG - 1 - step
        grad_out = grads[layer + 1, k]

        @pl.when(layer != r)
        def _():
            grad_ship(layer, k).start()

        x_float = acts[layer, k].astype(F32)
        inv_rms = inv_rms_of(x_float)
        x_hat = x_float * inv_rms
        gain = gains[layer, 0:1, :]
        grad_gelu = dot_nt(grad_out, wd[layer]).astype(BF16).astype(F32)
        grad_hidden = (grad_gelu * slopes[layer, k]).astype(BF16)
        grad_normed = dot_nt(grad_hidden, wu[layer]).astype(BF16).astype(F32)
        dg_part[layer] += fold_rows(grad_normed * x_hat)
        grad_hat = grad_normed * gain
        mean_dot = jnp.mean(grad_hat * x_hat, axis=-1, keepdims=True)
        grad_x = inv_rms * (grad_hat - x_hat * mean_dot)
        grads[layer, k] = (grad_out.astype(F32) + grad_x).astype(BF16)
        return k

    def bwd_chunk(k, carry):
        @pl.when(row < n_rows - 1)
        def _():
            rcopy(grads.at[SEG, k], grads.at[SEG, k], bwd_send, bwd_recv.at[k], me).wait_recv()

        lax.fori_loop(0, SEG, bwd_layer, k)

        @pl.when(row > 0)
        def _():
            rcopy(grads.at[0, k], grads.at[SEG, k], bwd_send, bwd_recv.at[k], me - SEG).start()
        return carry

    lax.fori_loop(0, N_CHUNKS, bwd_chunk, 0)

    def dg_ship(layer):
        return rcopy(dg_part.at[layer], dg_stash.at[r], dg_send, dg_recv, row_base + layer)

    for step in range(1, SEG):
        dg_ship(lax.rem(r + step, SEG)).start()
    dg_stash[r] = dg_part[r]

    @pl.when(row == n_rows - 1)
    def _():
        rest = loss_stash.at[pl.ds(0, SEG - 1)]
        rcopy(rest, rest, lrow_send, lrow_recv, me).wait_recv()
        loss_total[...] = jnp.sum(loss_stash[...], axis=0)
        for step in range(1, n_rows):
            rcopy(loss_total, loss_total, lcol_send, lcol_recv, me - step * SEG).start()

    act_stash[r] = acts[r]
    grad_stash[r] = grads[r + 1]
    rest = act_stash.at[pl.ds(0, SEG - 1)]
    rcopy(rest, rest, as_send, as_recv, me).wait_recv()
    rcopy(rest, rest, gs_send, gs_recv, me).wait_recv()
    dwu_ref[...] = jnp.zeros_like(dwu_ref)
    dwd_t[...] = jnp.zeros_like(dwd_t)

    def weight_block(src, carry):
        rows = N_CHUNKS * chunk
        x_float = act_stash[src].reshape(rows, d_model).astype(F32)
        grad_out = grad_stash[src].reshape(rows, d_model)
        normed = (x_float * inv_rms_of(x_float) * gains[r, 0:1, :]).astype(BF16)
        value, slope = gelu_parts(dot_nn(normed, wu[r]))
        grad_gelu = dot_nt(grad_out, wd[r]).astype(BF16).astype(F32)
        grad_hidden = (grad_gelu * slope).astype(BF16)
        dwu_ref[0] += dot_tn(normed, grad_hidden)
        dwd_t[...] += dot_tn(grad_out, value.astype(BF16))
        return carry

    lax.fori_loop(0, SEG, weight_block, 0)
    dwd_ref[0] = dwd_t[...].T

    rest_dg = dg_stash.at[pl.ds(0, SEG - 1)]
    rcopy(rest_dg, rest_dg, dg_send, dg_recv, me).wait_recv()
    dgain_ref[...] = jnp.sum(jnp.sum(dg_stash[...], axis=0), axis=0, keepdims=True)

    @pl.when(row < n_rows - 1)
    def _():
        rcopy(loss_total, loss_total, lcol_send, lcol_recv, me).wait_recv()
    loss_ref[0] = jnp.sum(loss_total[...]) * loss_scale

    rest_u = wu.at[pl.ds(0, SEG - 1)]
    rest_d = wd.at[pl.ds(0, SEG - 1)]
    rcopy(rest_u, rest_u, agu_send, gain_recv, me).wait_send()
    rcopy(rest_d, rest_d, agd_send, gain_recv, me).wait_send()
    rest_gain = gains.at[pl.ds(0, SEG - 1)]
    rcopy(rest_gain, rest_gain, gain_send, gain_recv, me).wait_send()
    rcopy(rest, rest, as_send, as_recv, me).wait_send()
    rcopy(rest, rest, gs_send, gs_recv, me).wait_send()
    rcopy(rest_dg, rest_dg, dg_send, dg_recv, me).wait_send()

    @pl.when(row < n_rows - 1)
    def _():
        rcopy(acts.at[0], acts.at[0], fwd_send, dg_recv, me).wait_send()

    @pl.when(row > 0)
    def _():
        rcopy(grads.at[0], grads.at[0], bwd_send, dg_recv, me).wait_send()

    @pl.when(row == n_rows - 1)
    def _():
        rest_row = loss_stash.at[pl.ds(0, SEG - 1)]
        rcopy(rest_row, rest_row, lrow_send, lrow_recv, me).wait_send()
        for step in range(1, n_rows):
            rcopy(loss_total, loss_total, lcol_send, lcol_recv, me).wait_send()


def solution(mesh):
    n_stages = mesh.shape['stage']

    def stage_body(x_in, y_target, w_up, w_down, norm_gain):
        n_micro, n_tok, d_model = x_in.shape
        d_ff = w_up.shape[2]
        n_rows = n_micro * n_tok
        chunk = n_rows // SEG // N_CHUNKS
        loss_scale = 1.0 / (n_rows * d_model)
        sem = pltpu.SemaphoreType.DMA
        act_shape = (N_CHUNKS, chunk, d_model)
        scratch = [
            pltpu.VMEM((SEG, d_model, d_ff), BF16),
            pltpu.VMEM((SEG, d_ff, d_model), BF16),
            pltpu.VMEM((SEG, 8, d_model), F32),
            pltpu.VMEM((SEG + 1,) + act_shape, BF16),
            pltpu.VMEM((SEG + 1,) + act_shape, BF16),
            pltpu.VMEM((SEG, N_CHUNKS, chunk, d_ff), F32),
            pltpu.VMEM((SEG,) + act_shape, BF16),
            pltpu.VMEM((SEG,) + act_shape, BF16),
            pltpu.VMEM(act_shape, BF16),
            pltpu.VMEM((d_model, d_ff), F32),
            pltpu.VMEM((SEG, 8, d_model), F32),
            pltpu.VMEM((SEG, 8, d_model), F32),
            pltpu.VMEM((8, d_model), F32),
            pltpu.VMEM((SEG, 8, d_model), F32),
            pltpu.VMEM((8, d_model), F32),
            sem((2,)), sem((N_CHUNKS,)), sem((N_CHUNKS,)),
            sem, sem((SEG,)), sem, sem((SEG,)), sem, sem,
            sem, sem, sem, sem, sem, sem((N_CHUNKS,)), sem, sem((N_CHUNKS,)),
            sem, sem, sem, sem, sem, sem,
        ]
        any_spec = pl.BlockSpec(memory_space=pl.ANY)
        vmem_spec = pl.BlockSpec(memory_space=pltpu.VMEM)
        dw_up, dw_down, dgain, loss = pl.pallas_call(
            functools.partial(step_kernel, n_stages, loss_scale),
            out_shape=(jax.ShapeDtypeStruct(w_up.shape, F32), jax.ShapeDtypeStruct(w_down.shape, F32),
                       jax.ShapeDtypeStruct(norm_gain.shape, F32), jax.ShapeDtypeStruct((1,), F32)),
            in_specs=[any_spec, any_spec, any_spec, any_spec, vmem_spec],
            out_specs=(vmem_spec, vmem_spec, vmem_spec, pl.BlockSpec(memory_space=pltpu.SMEM)),
            scratch_shapes=scratch,
            compiler_params=pltpu.CompilerParams(collective_id=0, has_side_effects=True,
                                                 vmem_limit_bytes=60 * 1024 * 1024),
        )(x_in.reshape(n_rows, d_model), y_target.reshape(n_rows, d_model), w_up, w_down, norm_gain)
        return dw_up, dw_down, dgain, loss

    return jax.shard_map(stage_body, mesh=mesh,
                         in_specs=(P('dp'), P('dp'), P('stage'), P('stage'), P('stage')),
                         out_specs=(P(('dp', 'stage')), P(('dp', 'stage')), P(('dp', 'stage')), P('dp')),
                         check_vma=False)
```

time: 3540 us -> 174 us (0.05); the launches traced: 3500 us -> 174 us
  loops' own time: 1010 us -> 0 us
  starting transfers between devices: 972 us -> 0 us
  matrix products: 681 us -> 0 us
  local copies, waits for them, and re-layouts: 554 us -> 3.93 us
  Pallas kernels: 0 us -> 167 us
  other arithmetic: 162 us -> 0 us
  blocking collectives: 96.6 us -> 0 us
    another operation x2 -> x0, loops' own time: 1010 us -> none  [the longest x1 748 us: stage_body(): fwd_out = lax.fori_loop(0, n_ticks, fwd_tick, fwd_init)]
    ppermute x258 -> x0, starting transfers between devices: 972 us -> none  [the longest x63 358 us: bwd_tick(): lax.ppermute(grad_act[1], 'stage', next_perm)]
    dot_general x378 -> x0, matrix products: 681 us -> none  [the longest x63 219 us: layer_backward(): jnp.einsum('zbd,zbf->zdf', normed, grad_hidden, preferred_element_type=jn...]
    slice x318 -> x0, local copies, waits for them, and re-layouts: 328 us -> none  [the longest x126 211 us: pick_pairs(): source[dir_idx]]
    pallas_call x0 -> x1, Pallas kernels: none -> 167 us  [stage_body(): pl.pallas_call(functools.partial(step_kernel, n_stages, loss_scale), out_...]
    dynamic_slice x189 -> x0, local copies, waits for them, and re-layouts: 102 us -> none  [the longest x63 51.9 us: pick_rows(): lax.dynamic_index_in_dim(source, row_idx[dir_idx], 0, keepdims=False)]
    psum x1 -> x0, blocking collectives: 96.6 us -> none  [stage_body(): loss_total = lax.psum(loss_sum, 'stage') * loss_scale]
    another operation x129 -> x0, other arithmetic: 91.7 us -> none  [the longest x63 88.2 us: bwd_tick(): jnp.stack([lax.ppermute(grad_act[0], 'stage', prev_perm), lax.ppermute(gr...]
where the time goes in v1:
time: 174 us
  Pallas kernels  167 us (96%)
  local copies, waits for them, and re-layouts  3.93 us (2%)
  between operations  2.41 us (1%)
    pallas_call x1, Pallas kernels, stage_body(): pl.pallas_call(functools.partial(step_kernel, n_stages, loss_scale), out_...  167 us
    unnamed x7, local copies, waits for them, and re-layouts  3.93 us

profile of v1, /device:TPU:97, one launch (start us, length us, event | category | flops | bytes accessed | tf_op | source)
XLA Modules:
  0.0 173.7 jit_solution(7715507708670517700)
XLA Ops:
  0.6 167.3 %shard_map.84 = (f32[1,256,1024]{2,1,0:T(8,128)}, f32[1,1024,256]{2,1,0:T(8,128)}, f32[1,256]{1,0:T(1,128)}, f32[1]{0:T(128)}) custom-call(bf16[4096,256]{1,0:T(8,128)(2,1)} %bitcast.2, bf16[4096,256]{1,0:T(8,128)(2,1)} %bitcast.3, bf16[1,256,1024]{2,1,0:T(8,128)(2,1)} %wu_hbm.1, bf16[1,1024,256]{2,1,0:T(8,128)(2,1)} %wd_hbm.1, f32[1,256]{1,0:T(1,128)} %gain_ref.1), custom_call_target="tpu_custom_call" | custom-call | tf_op jit(solution)/shard_map/pallas_call | solution.py:343
  168.0 0.0 copy-start
  168.0 0.0 copy-start.1
  168.0 2.4 %copy.13 = f32[1,256,1024]{2,1,0:T(8,128)} copy(f32[1,256,1024]{2,1,0:T(8,128)} %get-tuple-element.8) | data formatting | bytes 2097152
  170.4 0.0 copy-done
  170.4 1.0 copy.14
  171.4 0.0 copy-done.1
  171.4 0.6 copy.15
Async XLA Ops:
  168.0 2.4 %copy-start = (f32[1,1024,256]{2,1,0:T(8,128)S(1)}, f32[1,1024,256]{2,1,0:T(8,128)}, u32[]{:S(2)}) copy-start(f32[1,1024,256]{2,1,0:T(8,128)} %get-tuple-element.9) | copy-start | bytes 3145732
  168.0 3.4 %copy-start.1 = (f32[1,256]{1,0:T(1,128)S(1)}, f32[1,256]{1,0:T(1,128)}, u32[]{:S(2)}) copy-start(f32[1,256]{1,0:T(1,128)} %get-tuple-element.10) | copy-start | bytes 3076

commit v2 on v1

--- a/solution.py
+++ b/solution.py
@@ -10,6 +10,8 @@
 NORM_EPS = 1e-6
 SEG = 8
 N_CHUNKS = 4
+COLS = 256
+HALF = SEG // 2
 GELU_C = 0.7978845608028654
 GELU_A = 0.044715
 MESH = pl.DeviceIdType.MESH
@@ -29,13 +31,18 @@
     return lax.dot_general(lhs, rhs, (((0,), (0,)), ((), ())), preferred_element_type=F32)
 
 
-def gelu_parts(hidden):
+def gelu_gate(hidden):
     sq = hidden * hidden
-    tanh_val = jnp.tanh(hidden * (GELU_C + (GELU_C * GELU_A) * sq))
-    half = 0.5 * hidden
-    value = half + half * tanh_val
-    slope = (0.5 + 0.5 * tanh_val) + (half * (1.0 - tanh_val * tanh_val)) * (GELU_C + (3.0 * GELU_C * GELU_A) * sq)
-    return value, slope
+    gate = 0.5 + 0.5 * jnp.tanh(hidden * (GELU_C + (GELU_C * GELU_A) * sq))
+    return gate, sq
+
+
+def gelu_value(hidden):
+    return hidden * gelu_gate(hidden)[0]
+
+
+def gelu_slope(hidden, gate, sq):
+    return gate + ((gate * (1.0 - gate)) * hidden) * (2.0 * GELU_C + (6.0 * GELU_C * GELU_A) * sq)
 
 
 def inv_rms_of(x_float):
@@ -50,7 +57,7 @@
 def step_kernel(n_stages, loss_scale,
                 x_hbm, y_hbm, wu_hbm, wd_hbm, gain_ref,
                 dwu_ref, dwd_ref, dgain_ref, loss_ref,
-                wu, wd, gains, acts, grads, slopes, act_stash, grad_stash, targets, dwd_t,
+                wu, wd, gains, acts, grads, hiddens, act_stash, grad_stash, value_stash, slope_stash, targets, dwd_t,
                 dg_part, dg_stash, loss_part, loss_stash, loss_total,
                 load_sem, x_sem, y_sem, agu_send, agu_recv, agd_send, agd_recv, gain_send, gain_recv,
                 as_send, as_recv, gs_send, gs_recv, fwd_send, fwd_recv, bwd_send, bwd_recv,
@@ -103,12 +110,13 @@
     dg_part[...] = jnp.zeros_like(dg_part)
     loss_part[...] = jnp.zeros_like(loss_part)
 
-    barrier = pltpu.get_barrier_semaphore()
-    for step in range(1, SEG):
-        pl.semaphore_signal(barrier, inc=1, device_id={'stage': row_base + lax.rem(r + step, SEG)}, device_id_type=MESH)
-    for step in range(1, n_rows):
-        pl.semaphore_signal(barrier, inc=1, device_id={'stage': lax.rem(row + step, n_rows) * SEG + r}, device_id_type=MESH)
-    pl.semaphore_wait(barrier, SEG - 1 + n_rows - 1)
+    with jax.named_scope('barrier'):
+        barrier = pltpu.get_barrier_semaphore()
+        for step in range(1, SEG):
+            pl.semaphore_signal(barrier, inc=1, device_id={'stage': row_base + lax.rem(r + step, SEG)}, device_id_type=MESH)
+        for step in range(1, n_rows):
+            pl.semaphore_signal(barrier, inc=1, device_id={'stage': lax.rem(row + step, n_rows) * SEG + r}, device_id_type=MESH)
+        pl.semaphore_wait(barrier, SEG - 1 + n_rows - 1)
 
     def u_copy(slot, dev):
         return rcopy(wu.at[slot], wu.at[slot], agu_send, agu_recv.at[slot], row_base + dev)
@@ -116,8 +124,10 @@
     def d_copy(slot, dev):
         return rcopy(wd.at[slot], wd.at[slot], agd_send, agd_recv.at[slot], row_base + dev)
 
-    load_u.wait()
-    load_d.wait()
+    with jax.named_scope('w_load_u'):
+        load_u.wait()
+    with jax.named_scope('w_load_d'):
+        load_d.wait()
     u_copy(r, right).start()
     d_copy(r, left).start()
     d_copy(r, right).start()
@@ -127,38 +137,47 @@
     for step in range(1, SEG):
         rcopy(gains.at[r], gains.at[r], gain_send, gain_recv, row_base + lax.rem(r + step, SEG)).start()
 
-    u_copy(left, r).wait_recv()
+    with jax.named_scope('ag_u_left'):
+        u_copy(left, r).wait_recv()
     u_copy(left, right).start()
     u_copy(left, sib).start()
-    d_copy(right, r).wait_recv()
+    with jax.named_scope('ag_d_right'):
+        d_copy(right, r).wait_recv()
     d_copy(right, left).start()
     d_copy(right, sib).start()
-    d_copy(left, r).wait_recv()
+    with jax.named_scope('ag_d_left'):
+        d_copy(left, r).wait_recv()
     d_copy(left, sib).start()
-    u_copy(right, r).wait_recv()
+    with jax.named_scope('ag_u_right'):
+        u_copy(right, r).wait_recv()
     u_copy(right, sib).start()
-    u_copy(across, r).wait_recv()
+    with jax.named_scope('ag_u_across'):
+        u_copy(across, r).wait_recv()
     u_copy(across, sib).start()
-    d_copy(across, r).wait_recv()
+    with jax.named_scope('ag_d_across'):
+        d_copy(across, r).wait_recv()
     d_copy(across, sib).start()
-    for slot in (sib, left + flip, right + flip, across + flip):
-        u_copy(slot, r).wait_recv()
-        d_copy(slot, r).wait_recv()
+    with jax.named_scope('ag_sib'):
+        for slot in (sib, left + flip, right + flip, across + flip):
+            u_copy(slot, r).wait_recv()
+            d_copy(slot, r).wait_recv()
     rcopy(gains.at[pl.ds(0, SEG - 1)], gains.at[pl.ds(0, SEG - 1)], gain_send, gain_recv, me).wait_recv()
 
     def act_ship(layer, k):
-        return rcopy(acts.at[layer, k], act_stash.at[r, k], as_send, as_recv, row_base + layer)
+        return rcopy(acts.at[layer, k], act_stash.at[k, r], as_send, as_recv, row_base + layer)
 
     def grad_ship(layer, k):
-        return rcopy(grads.at[layer + 1, k], grad_stash.at[r, k], gs_send, gs_recv, row_base + layer)
+        return rcopy(grads.at[layer + 1, k], grad_stash.at[k, r], gs_send, gs_recv.at[k], row_base + layer)
 
     def fwd_layer(layer, k):
         x_float = acts[layer, k].astype(F32)
         normed = (x_float * inv_rms_of(x_float) * gains[layer, 0:1, :]).astype(BF16)
-        hidden = dot_nn(normed, wu[layer])
-        value, slope = gelu_parts(hidden)
-        slopes[layer, k] = slope
-        out = x_float + dot_nn(value.astype(BF16), wd[layer])
+        out = x_float
+        for part in range(0, d_ff, COLS):
+            cols = slice(part, part + COLS)
+            hidden = dot_nn(normed, wu[layer, :, cols])
+            hiddens[layer, k, :, cols] = hidden
+            out += dot_nn(gelu_value(hidden).astype(BF16), wd[layer, cols, :])
         acts[layer + 1, k] = out.astype(BF16)
 
         @pl.when(layer != r)
@@ -173,9 +192,11 @@
 
         @pl.when(row > 0)
         def _():
-            rcopy(acts.at[0, k], acts.at[0, k], fwd_send, fwd_recv.at[k], me).wait_recv()
-
-        lax.fori_loop(0, SEG, fwd_layer, k)
+            with jax.named_scope('fwd_wait'):
+                rcopy(acts.at[0, k], acts.at[0, k], fwd_send, fwd_recv.at[k], me).wait_recv()
+
+        with jax.named_scope('fwd_layers'):
+            lax.fori_loop(0, SEG, fwd_layer, k)
 
         @pl.when(row < n_rows - 1)
         def _():
@@ -197,6 +218,39 @@
         for step in range(1, SEG):
             rcopy(loss_stash.at[r], loss_stash.at[r], lrow_send, lrow_recv, row_base + lax.rem(r + step, SEG)).start()
 
+    rest = act_stash.at[0, pl.ds(0, SEG - 1)]
+    all_rest = acts.at[pl.ds(0, SEG - 1)]
+
+    def owner_block(index):
+        return lax.div(index, 2), pl.ds(lax.rem(index, 2) * HALF, HALF)
+
+    def value_block(index, carry):
+        k, srcs = owner_block(index)
+        x_float = act_stash[k, srcs].reshape(HALF * chunk, d_model).astype(F32)
+        normed = (x_float * inv_rms_of(x_float) * gains[r, 0:1, :]).astype(BF16)
+        act_stash[k, srcs] = normed.reshape(HALF, chunk, d_model)
+        for part in range(0, d_ff, COLS):
+            cols = slice(part, part + COLS)
+            hidden = dot_nn(normed, wu[r, :, cols])
+            gate, sq = gelu_gate(hidden)
+            value_stash[k, srcs, :, cols] = (hidden * gate).astype(BF16).reshape(HALF, chunk, COLS)
+            slope_stash[k, srcs, :, cols] = gelu_slope(hidden, gate, sq).reshape(HALF, chunk, COLS)
+        return carry
+
+    def value_phase():
+        with jax.named_scope('as_wait'):
+            rcopy(all_rest, all_rest, as_send, as_recv, me).wait_recv()
+        for k in range(N_CHUNKS):
+            act_stash[k, r] = acts[r, k]
+        dwu_ref[...] = jnp.zeros_like(dwu_ref)
+        dwd_t[...] = jnp.zeros_like(dwd_t)
+        with jax.named_scope('value_blocks'):
+            lax.fori_loop(0, 2 * N_CHUNKS, value_block, 0)
+
+    @pl.when(row < n_rows - 1)
+    def _():
+        value_phase()
+
     def bwd_layer(step, k):
         layer = SEG - 1 - step
         grad_out = grads[layer + 1, k]
@@ -209,9 +263,15 @@
         inv_rms = inv_rms_of(x_float)
         x_hat = x_float * inv_rms
         gain = gains[layer, 0:1, :]
-        grad_gelu = dot_nt(grad_out, wd[layer]).astype(BF16).astype(F32)
-        grad_hidden = (grad_gelu * slopes[layer, k]).astype(BF16)
-        grad_normed = dot_nt(grad_hidden, wu[layer]).astype(BF16).astype(F32)
+        grad_normed = 0.0
+        for part in range(0, d_ff, COLS):
+            cols = slice(part, part + COLS)
+            hidden = hiddens[layer, k, :, cols]
+            slope = gelu_slope(hidden, *gelu_gate(hidden))
+            grad_gelu = dot_nt(grad_out, wd[layer, cols, :]).astype(BF16).astype(F32)
+            grad_hidden = (grad_gelu * slope).astype(BF16)
+            grad_normed += dot_nt(grad_hidden, wu[layer, :, cols])
+        grad_normed = grad_normed.astype(BF16).astype(F32)
         dg_part[layer] += fold_rows(grad_normed * x_hat)
         grad_hat = grad_normed * gain
         mean_dot = jnp.mean(grad_hat * x_hat, axis=-1, keepdims=True)
@@ -222,9 +282,11 @@
     def bwd_chunk(k, carry):
         @pl.when(row < n_rows - 1)
         def _():
-            rcopy(grads.at[SEG, k], grads.at[SEG, k], bwd_send, bwd_recv.at[k], me).wait_recv()
-
-        lax.fori_loop(0, SEG, bwd_layer, k)
+            with jax.named_scope('bwd_wait'):
+                rcopy(grads.at[SEG, k], grads.at[SEG, k], bwd_send, bwd_recv.at[k], me).wait_recv()
+
+        with jax.named_scope('bwd_layers'):
+            lax.fori_loop(0, SEG, bwd_layer, k)
 
         @pl.when(row > 0)
         def _():
@@ -248,31 +310,39 @@
         for step in range(1, n_rows):
             rcopy(loss_total, loss_total, lcol_send, lcol_recv, me - step * SEG).start()
 
-    act_stash[r] = acts[r]
-    grad_stash[r] = grads[r + 1]
-    rest = act_stash.at[pl.ds(0, SEG - 1)]
-    rcopy(rest, rest, as_send, as_recv, me).wait_recv()
-    rcopy(rest, rest, gs_send, gs_recv, me).wait_recv()
-    dwu_ref[...] = jnp.zeros_like(dwu_ref)
-    dwd_t[...] = jnp.zeros_like(dwd_t)
-
-    def weight_block(src, carry):
-        rows = N_CHUNKS * chunk
-        x_float = act_stash[src].reshape(rows, d_model).astype(F32)
-        grad_out = grad_stash[src].reshape(rows, d_model)
-        normed = (x_float * inv_rms_of(x_float) * gains[r, 0:1, :]).astype(BF16)
-        value, slope = gelu_parts(dot_nn(normed, wu[r]))
-        grad_gelu = dot_nt(grad_out, wd[r]).astype(BF16).astype(F32)
-        grad_hidden = (grad_gelu * slope).astype(BF16)
-        dwu_ref[0] += dot_tn(normed, grad_hidden)
-        dwd_t[...] += dot_tn(grad_out, value.astype(BF16))
+    @pl.when(row == n_rows - 1)
+    def _():
+        value_phase()
+
+    for k in range(N_CHUNKS):
+        grad_stash[k, r] = grads[r + 1, k]
+
+    def weight_block(index, carry):
+        k, srcs = owner_block(index)
+        rows = HALF * chunk
+
+        @pl.when(lax.rem(index, 2) == 0)
+        def _():
+            with jax.named_scope('gs_wait'):
+                rcopy(rest, rest, gs_send, gs_recv.at[k], me).wait_recv()
+        normed = act_stash[k, srcs].reshape(rows, d_model)
+        grad_out = grad_stash[k, srcs].reshape(rows, d_model)
+        for part in range(0, d_ff, COLS):
+            cols = slice(part, part + COLS)
+            grad_gelu = dot_nt(grad_out, wd[r, cols, :]).astype(BF16).astype(F32)
+            grad_hidden = (grad_gelu * slope_stash[k, srcs, :, cols].reshape(rows, COLS)).astype(BF16)
+            dwu_ref[0, :, cols] += dot_tn(normed, grad_hidden)
+            dwd_t[:, cols] += dot_tn(grad_out, value_stash[k, srcs, :, cols].reshape(rows, COLS))
         return carry
 
-    lax.fori_loop(0, SEG, weight_block, 0)
-    dwd_ref[0] = dwd_t[...].T
+    with jax.named_scope('weight_blocks'):
+        lax.fori_loop(0, 2 * N_CHUNKS, weight_block, 0)
+    with jax.named_scope('turn'):
+        dwd_ref[0] = dwd_t[...].T
 
     rest_dg = dg_stash.at[pl.ds(0, SEG - 1)]
-    rcopy(rest_dg, rest_dg, dg_send, dg_recv, me).wait_recv()
+    with jax.named_scope('dg_wait'):
+        rcopy(rest_dg, rest_dg, dg_send, dg_recv, me).wait_recv()
     dgain_ref[...] = jnp.sum(jnp.sum(dg_stash[...], axis=0), axis=0, keepdims=True)
 
     @pl.when(row < n_rows - 1)
@@ -286,8 +356,8 @@
     rcopy(rest_d, rest_d, agd_send, gain_recv, me).wait_send()
     rest_gain = gains.at[pl.ds(0, SEG - 1)]
     rcopy(rest_gain, rest_gain, gain_send, gain_recv, me).wait_send()
-    rcopy(rest, rest, as_send, as_recv, me).wait_send()
-    rcopy(rest, rest, gs_send, gs_recv, me).wait_send()
+    rcopy(all_rest, all_rest, as_send, dg_recv, me).wait_send()
+    rcopy(all_rest, all_rest, gs_send, dg_recv, me).wait_send()
     rcopy(rest_dg, rest_dg, dg_send, dg_recv, me).wait_send()
 
     @pl.when(row < n_rows - 1)
@@ -324,8 +394,10 @@
             pltpu.VMEM((SEG + 1,) + act_shape, BF16),
             pltpu.VMEM((SEG + 1,) + act_shape, BF16),
             pltpu.VMEM((SEG, N_CHUNKS, chunk, d_ff), F32),
-            pltpu.VMEM((SEG,) + act_shape, BF16),
-            pltpu.VMEM((SEG,) + act_shape, BF16),
+            pltpu.VMEM((N_CHUNKS, SEG, chunk, d_model), BF16),
+            pltpu.VMEM((N_CHUNKS, SEG, chunk, d_model), BF16),
+            pltpu.VMEM((N_CHUNKS, SEG, chunk, d_ff), BF16),
+            pltpu.VMEM((N_CHUNKS, SEG, chunk, d_ff), F32),
             pltpu.VMEM(act_shape, BF16),
             pltpu.VMEM((d_model, d_ff), F32),
             pltpu.VMEM((SEG, 8, d_model), F32),
@@ -335,7 +407,7 @@
             pltpu.VMEM((8, d_model), F32),
             sem((2,)), sem((N_CHUNKS,)), sem((N_CHUNKS,)),
             sem, sem((SEG,)), sem, sem((SEG,)), sem, sem,
-            sem, sem, sem, sem, sem, sem((N_CHUNKS,)), sem, sem((N_CHUNKS,)),
+            sem, sem, sem, sem((N_CHUNKS,)), sem, sem((N_CHUNKS,)), sem, sem((N_CHUNKS,)),
             sem, sem, sem, sem, sem, sem,
         ]
         any_spec = pl.BlockSpec(memory_space=pl.ANY)
@@ -348,7 +420,7 @@
             out_specs=(vmem_spec, vmem_spec, vmem_spec, pl.BlockSpec(memory_space=pltpu.SMEM)),
             scratch_shapes=scratch,
             compiler_params=pltpu.CompilerParams(collective_id=0, has_side_effects=True,
-                                                 vmem_limit_bytes=60 * 1024 * 1024),
+                                                 vmem_limit_bytes=67043328),
         )(x_in.reshape(n_rows, d_model), y_target.reshape(n_rows, d_model), w_up, w_down, norm_gain)
         return dw_up, dw_down, dgain, loss
 

time: 174 us -> 159 us (0.914)
  Pallas kernels: 167 us -> 152 us
    pallas_call x1, Pallas kernels: 167 us -> 152 us  [stage_body(): pl.pallas_call(functools.partial(step_kernel, n_stages, loss_scale), out_...]
where the time goes in v2:
time: 159 us; the launch traced here: 158 us
  Pallas kernels  152 us (96%)
  local copies, waits for them, and re-layouts  3.93 us (2%)
  between operations  2.41 us (2%)
    pallas_call x1, Pallas kernels, stage_body(): pl.pallas_call(functools.partial(step_kernel, n_stages, loss_scale), out_...  152 us
    unnamed x7, local copies, waits for them, and re-layouts  3.93 us

profile of v2, /device:TPU:97, one launch (start us, length us, event | category | flops | bytes accessed | tf_op | source)
XLA Modules:
  0.0 158.4 jit_solution(6303890666494474070)
XLA Ops:
  0.6 152.1 %shard_map.84 = (f32[1,256,1024]{2,1,0:T(8,128)}, f32[1,1024,256]{2,1,0:T(8,128)}, f32[1,256]{1,0:T(1,128)}, f32[1]{0:T(128)}) custom-call(bf16[4096,256]{1,0:T(8,128)(2,1)} %bitcast.2, bf16[4096,256]{1,0:T(8,128)(2,1)} %bitcast.3, bf16[1,256,1024]{2,1,0:T(8,128)(2,1)} %wu_hbm.1, bf16[1,1024,256]{2,1,0:T(8,128)(2,1)} %wd_hbm.1, f32[1,256]{1,0:T(1,128)} %gain_ref.1), custom_call_target="tpu_custom_call" | custom-call | tf_op jit(solution)/shard_map/pallas_call | solution.py:415
  152.7 0.0 copy-start
  152.7 0.0 copy-start.1
  152.7 2.4 %copy.13 = f32[1,256,1024]{2,1,0:T(8,128)} copy(f32[1,256,1024]{2,1,0:T(8,128)} %get-tuple-element.8) | data formatting | bytes 2097152
  155.1 0.0 copy-done
  155.1 1.0 copy.14
  156.1 0.0 copy-done.1
  156.1 0.6 copy.15
Async XLA Ops:
  152.7 2.4 %copy-start = (f32[1,1024,256]{2,1,0:T(8,128)S(1)}, f32[1,1024,256]{2,1,0:T(8,128)}, u32[]{:S(2)}) copy-start(f32[1,1024,256]{2,1,0:T(8,128)} %get-tuple-element.9) | copy-start | bytes 3145732
  152.7 3.4 %copy-start.1 = (f32[1,256]{1,0:T(1,128)S(1)}, f32[1,256]{1,0:T(1,128)}, u32[]{:S(2)}) copy-start(f32[1,256]{1,0:T(1,128)} %get-tuple-element.10) | copy-start | bytes 3076

commit v3 on v2

--- a/solution.py
+++ b/solution.py
@@ -12,6 +12,8 @@
 N_CHUNKS = 4
 COLS = 256
 HALF = SEG // 2
+UNROLL = 4
+BOTH_UNROLL = 2
 GELU_C = 0.7978845608028654
 GELU_A = 0.044715
 MESH = pl.DeviceIdType.MESH
@@ -164,10 +166,14 @@
     rcopy(gains.at[pl.ds(0, SEG - 1)], gains.at[pl.ds(0, SEG - 1)], gain_send, gain_recv, me).wait_recv()
 
     def act_ship(layer, k):
-        return rcopy(acts.at[layer, k], act_stash.at[k, r], as_send, as_recv, row_base + layer)
+        mine = layer == r
+        return rcopy(acts.at[layer, k], act_stash.at[k, jnp.where(mine, SEG, r)], as_send, as_recv,
+                     row_base + jnp.where(mine, sib, layer))
 
     def grad_ship(layer, k):
-        return rcopy(grads.at[layer + 1, k], grad_stash.at[k, r], gs_send, gs_recv.at[k], row_base + layer)
+        mine = layer == r
+        return rcopy(grads.at[layer + 1, k], grad_stash.at[k, jnp.where(mine, SEG, r)], gs_send, gs_recv.at[k],
+                     row_base + jnp.where(mine, sib, layer))
 
     def fwd_layer(layer, k):
         x_float = acts[layer, k].astype(F32)
@@ -179,13 +185,9 @@
             hiddens[layer, k, :, cols] = hidden
             out += dot_nn(gelu_value(hidden).astype(BF16), wd[layer, cols, :])
         acts[layer + 1, k] = out.astype(BF16)
-
-        @pl.when(layer != r)
-        def _():
-            act_ship(layer, k).start()
         return k
 
-    def fwd_chunk(k, carry):
+    def fwd_input_wait(k):
         @pl.when(row == 0)
         def _():
             x_load(k).wait()
@@ -195,70 +197,33 @@
             with jax.named_scope('fwd_wait'):
                 rcopy(acts.at[0, k], acts.at[0, k], fwd_send, fwd_recv.at[k], me).wait_recv()
 
+    def top_grad(k):
+        y_load(k).wait()
+        error_val = acts[SEG, k].astype(F32) - targets[k].astype(F32)
+        loss_part[...] += fold_rows(error_val * error_val)
+        grads[SEG, k] = ((2.0 * loss_scale) * error_val).astype(BF16)
+
+    def fwd_chunk(k, carry):
+        fwd_input_wait(k)
         with jax.named_scope('fwd_layers'):
-            lax.fori_loop(0, SEG, fwd_layer, k)
+            lax.fori_loop(0, SEG, fwd_layer, k, unroll=UNROLL)
 
         @pl.when(row < n_rows - 1)
         def _():
             rcopy(acts.at[SEG, k], acts.at[0, k], fwd_send, fwd_recv.at[k], me + SEG).start()
+        for layer in range(SEG):
+            act_ship(layer, k).start()
 
         @pl.when(row == n_rows - 1)
         def _():
-            y_load(k).wait()
-            error_val = acts[SEG, k].astype(F32) - targets[k].astype(F32)
-            loss_part[...] += fold_rows(error_val * error_val)
-            grads[SEG, k] = ((2.0 * loss_scale) * error_val).astype(BF16)
+            top_grad(k)
         return carry
 
-    lax.fori_loop(0, N_CHUNKS, fwd_chunk, 0)
-
-    @pl.when(row == n_rows - 1)
-    def _():
-        loss_stash[r] = loss_part[...]
-        for step in range(1, SEG):
-            rcopy(loss_stash.at[r], loss_stash.at[r], lrow_send, lrow_recv, row_base + lax.rem(r + step, SEG)).start()
-
-    rest = act_stash.at[0, pl.ds(0, SEG - 1)]
-    all_rest = acts.at[pl.ds(0, SEG - 1)]
-
-    def owner_block(index):
-        return lax.div(index, 2), pl.ds(lax.rem(index, 2) * HALF, HALF)
-
-    def value_block(index, carry):
-        k, srcs = owner_block(index)
-        x_float = act_stash[k, srcs].reshape(HALF * chunk, d_model).astype(F32)
-        normed = (x_float * inv_rms_of(x_float) * gains[r, 0:1, :]).astype(BF16)
-        act_stash[k, srcs] = normed.reshape(HALF, chunk, d_model)
-        for part in range(0, d_ff, COLS):
-            cols = slice(part, part + COLS)
-            hidden = dot_nn(normed, wu[r, :, cols])
-            gate, sq = gelu_gate(hidden)
-            value_stash[k, srcs, :, cols] = (hidden * gate).astype(BF16).reshape(HALF, chunk, COLS)
-            slope_stash[k, srcs, :, cols] = gelu_slope(hidden, gate, sq).reshape(HALF, chunk, COLS)
-        return carry
-
-    def value_phase():
-        with jax.named_scope('as_wait'):
-            rcopy(all_rest, all_rest, as_send, as_recv, me).wait_recv()
-        for k in range(N_CHUNKS):
-            act_stash[k, r] = acts[r, k]
-        dwu_ref[...] = jnp.zeros_like(dwu_ref)
-        dwd_t[...] = jnp.zeros_like(dwd_t)
-        with jax.named_scope('value_blocks'):
-            lax.fori_loop(0, 2 * N_CHUNKS, value_block, 0)
-
-    @pl.when(row < n_rows - 1)
-    def _():
-        value_phase()
+    lax.fori_loop(0, jnp.where(row == n_rows - 1, 1, N_CHUNKS), fwd_chunk, 0)
 
     def bwd_layer(step, k):
         layer = SEG - 1 - step
         grad_out = grads[layer + 1, k]
-
-        @pl.when(layer != r)
-        def _():
-            grad_ship(layer, k).start()
-
         x_float = acts[layer, k].astype(F32)
         inv_rms = inv_rms_of(x_float)
         x_hat = x_float * inv_rms
@@ -279,6 +244,68 @@
         grads[layer, k] = (grad_out.astype(F32) + grad_x).astype(BF16)
         return k
 
+    def bwd_output(k):
+        @pl.when(row > 0)
+        def _():
+            rcopy(grads.at[0, k], grads.at[SEG, k], bwd_send, bwd_recv.at[k], me - SEG).start()
+        for layer in range(SEG):
+            grad_ship(layer, k).start()
+
+    def both_layers(step, k):
+        fwd_layer(step, k)
+        bwd_layer(step, k - 1)
+        return k
+
+    def both_chunks(k, carry):
+        fwd_input_wait(k)
+        with jax.named_scope('both_layers'):
+            lax.fori_loop(0, SEG, both_layers, k, unroll=BOTH_UNROLL)
+        bwd_output(k - 1)
+        top_grad(k)
+        for layer in range(SEG):
+            act_ship(layer, k).start()
+        return carry
+
+    @pl.when(row == n_rows - 1)
+    def _():
+        lax.fori_loop(1, N_CHUNKS, both_chunks, 0)
+        loss_stash[r] = loss_part[...]
+        for step in range(1, SEG):
+            rcopy(loss_stash.at[r], loss_stash.at[r], lrow_send, lrow_recv, row_base + lax.rem(r + step, SEG)).start()
+
+    rest = act_stash.at[0, pl.ds(0, SEG)]
+    all_rest = acts.at[pl.ds(0, SEG)]
+
+    def owner_block(index):
+        return lax.div(index, 2), pl.ds(lax.rem(index, 2) * HALF, HALF)
+
+    def value_block(index, carry):
+        k, srcs = owner_block(index)
+        x_float = act_stash[k, srcs].reshape(HALF * chunk, d_model).astype(F32)
+        normed = (x_float * inv_rms_of(x_float) * gains[r, 0:1, :]).astype(BF16)
+        act_stash[k, srcs] = normed.reshape(HALF, chunk, d_model)
+        for part in range(0, d_ff, COLS):
+            cols = slice(part, part + COLS)
+            hidden = dot_nn(normed, wu[r, :, cols])
+            gate, sq = gelu_gate(hidden)
+            value_stash[k, srcs, :, cols] = (hidden * gate).astype(BF16).reshape(HALF, chunk, COLS)
+            slope_stash[k, srcs, :, cols] = gelu_slope(hidden, gate, sq).reshape(HALF, chunk, COLS)
+        return carry
+
+    def value_phase():
+        with jax.named_scope('as_wait'):
+            rcopy(all_rest, all_rest, as_send, as_recv, me).wait_recv()
+        for k in range(N_CHUNKS):
+            act_stash[k, r] = acts[r, k]
+        dwu_ref[...] = jnp.zeros_like(dwu_ref)
+        dwd_t[...] = jnp.zeros_like(dwd_t)
+        with jax.named_scope('value_blocks'):
+            lax.fori_loop(0, 2 * N_CHUNKS, value_block, 0)
+
+    @pl.when(row < n_rows - 1)
+    def _():
+        value_phase()
+
     def bwd_chunk(k, carry):
         @pl.when(row < n_rows - 1)
         def _():
@@ -286,14 +313,11 @@
                 rcopy(grads.at[SEG, k], grads.at[SEG, k], bwd_send, bwd_recv.at[k], me).wait_recv()
 
         with jax.named_scope('bwd_layers'):
-            lax.fori_loop(0, SEG, bwd_layer, k)
-
-        @pl.when(row > 0)
-        def _():
-            rcopy(grads.at[0, k], grads.at[SEG, k], bwd_send, bwd_recv.at[k], me - SEG).start()
+            lax.fori_loop(0, SEG, bwd_layer, k, unroll=UNROLL)
+        bwd_output(k)
         return carry
 
-    lax.fori_loop(0, N_CHUNKS, bwd_chunk, 0)
+    lax.fori_loop(jnp.where(row == n_rows - 1, N_CHUNKS - 1, 0), N_CHUNKS, bwd_chunk, 0)
 
     def dg_ship(layer):
         return rcopy(dg_part.at[layer], dg_stash.at[r], dg_send, dg_recv, row_base + layer)
@@ -317,26 +341,22 @@
     for k in range(N_CHUNKS):
         grad_stash[k, r] = grads[r + 1, k]
 
-    def weight_block(index, carry):
-        k, srcs = owner_block(index)
-        rows = HALF * chunk
-
-        @pl.when(lax.rem(index, 2) == 0)
-        def _():
-            with jax.named_scope('gs_wait'):
-                rcopy(rest, rest, gs_send, gs_recv.at[k], me).wait_recv()
-        normed = act_stash[k, srcs].reshape(rows, d_model)
-        grad_out = grad_stash[k, srcs].reshape(rows, d_model)
+    def weight_block(k, carry):
+        rows = SEG * chunk
+        with jax.named_scope('gs_wait'):
+            rcopy(rest, rest, gs_send, gs_recv.at[k], me).wait_recv()
+        normed = act_stash[k, pl.ds(0, SEG)].reshape(rows, d_model)
+        grad_out = grad_stash[k, pl.ds(0, SEG)].reshape(rows, d_model)
         for part in range(0, d_ff, COLS):
             cols = slice(part, part + COLS)
             grad_gelu = dot_nt(grad_out, wd[r, cols, :]).astype(BF16).astype(F32)
-            grad_hidden = (grad_gelu * slope_stash[k, srcs, :, cols].reshape(rows, COLS)).astype(BF16)
+            grad_hidden = (grad_gelu * slope_stash[k, :, :, cols].reshape(rows, COLS)).astype(BF16)
             dwu_ref[0, :, cols] += dot_tn(normed, grad_hidden)
-            dwd_t[:, cols] += dot_tn(grad_out, value_stash[k, srcs, :, cols].reshape(rows, COLS))
+            dwd_t[:, cols] += dot_tn(grad_out, value_stash[k, :, :, cols].reshape(rows, COLS))
         return carry
 
     with jax.named_scope('weight_blocks'):
-        lax.fori_loop(0, 2 * N_CHUNKS, weight_block, 0)
+        lax.fori_loop(0, N_CHUNKS, weight_block, 0)
     with jax.named_scope('turn'):
         dwd_ref[0] = dwd_t[...].T
 
@@ -394,8 +414,8 @@
             pltpu.VMEM((SEG + 1,) + act_shape, BF16),
             pltpu.VMEM((SEG + 1,) + act_shape, BF16),
             pltpu.VMEM((SEG, N_CHUNKS, chunk, d_ff), F32),
-            pltpu.VMEM((N_CHUNKS, SEG, chunk, d_model), BF16),
-            pltpu.VMEM((N_CHUNKS, SEG, chunk, d_model), BF16),
+            pltpu.VMEM((N_CHUNKS, SEG + 1, chunk, d_model), BF16),
+            pltpu.VMEM((N_CHUNKS, SEG + 1, chunk, d_model), BF16),
             pltpu.VMEM((N_CHUNKS, SEG, chunk, d_ff), BF16),
             pltpu.VMEM((N_CHUNKS, SEG, chunk, d_ff), F32),
             pltpu.VMEM(act_shape, BF16),

time: 159 us -> 158 us (level)
  no operation moved by 1% of the time
where the time goes in v3:
time: 158 us
  Pallas kernels  152 us (96%)
  local copies, waits for them, and re-layouts  3.93 us (2%)
  between operations  2.41 us (2%)
    pallas_call x1, Pallas kernels, stage_body(): pl.pallas_call(functools.partial(step_kernel, n_stages, loss_scale), out_...  152 us
    unnamed x7, local copies, waits for them, and re-layouts  3.93 us

profile of v3, /device:TPU:97, one launch (start us, length us, event | category | flops | bytes accessed | tf_op | source)
XLA Modules:
  0.0 158.1 jit_solution(16608816046063027244)
XLA Ops:
  0.6 151.8 %shard_map.84 = (f32[1,256,1024]{2,1,0:T(8,128)}, f32[1,1024,256]{2,1,0:T(8,128)}, f32[1,256]{1,0:T(1,128)}, f32[1]{0:T(128)}) custom-call(bf16[4096,256]{1,0:T(8,128)(2,1)} %bitcast.2, bf16[4096,256]{1,0:T(8,128)(2,1)} %bitcast.3, bf16[1,256,1024]{2,1,0:T(8,128)(2,1)} %wu_hbm.1, bf16[1,1024,256]{2,1,0:T(8,128)(2,1)} %wd_hbm.1, f32[1,256]{1,0:T(1,128)} %gain_ref.1), custom_call_target="tpu_custom_call" | custom-call | tf_op jit(solution)/shard_map/pallas_call | solution.py:435
  152.4 0.0 copy-start
  152.4 0.0 copy-start.1
  152.4 2.4 %copy.13 = f32[1,256,1024]{2,1,0:T(8,128)} copy(f32[1,256,1024]{2,1,0:T(8,128)} %get-tuple-element.8) | data formatting | bytes 2097152
  154.8 0.0 copy-done
  154.8 1.0 copy.14
  155.8 0.0 copy-done.1
  155.8 0.6 copy.15
Async XLA Ops:
  152.4 2.4 %copy-start = (f32[1,1024,256]{2,1,0:T(8,128)S(1)}, f32[1,1024,256]{2,1,0:T(8,128)}, u32[]{:S(2)}) copy-start(f32[1,1024,256]{2,1,0:T(8,128)} %get-tuple-element.9) | copy-start | bytes 3145732
  152.4 3.4 %copy-start.1 = (f32[1,256]{1,0:T(1,128)S(1)}, f32[1,256]{1,0:T(1,128)}, u32[]{:S(2)}) copy-start(f32[1,256]{1,0:T(1,128)} %get-tuple-element.10) | copy-start | bytes 3076

commit v4 on v3

--- a/solution.py
+++ b/solution.py
@@ -12,8 +12,8 @@
 N_CHUNKS = 4
 COLS = 256
 HALF = SEG // 2
-UNROLL = 4
-BOTH_UNROLL = 2
+GROUP = 4
+LATE_ROWS = 2
 GELU_C = 0.7978845608028654
 GELU_A = 0.044715
 MESH = pl.DeviceIdType.MESH
@@ -185,7 +185,6 @@
             hiddens[layer, k, :, cols] = hidden
             out += dot_nn(gelu_value(hidden).astype(BF16), wd[layer, cols, :])
         acts[layer + 1, k] = out.astype(BF16)
-        return k
 
     def fwd_input_wait(k):
         @pl.when(row == 0)
@@ -203,10 +202,15 @@
         loss_part[...] += fold_rows(error_val * error_val)
         grads[SEG, k] = ((2.0 * loss_scale) * error_val).astype(BF16)
 
+    def fwd_group(group, k):
+        for step in range(GROUP):
+            fwd_layer(group * GROUP + step, k)
+        return k
+
     def fwd_chunk(k, carry):
         fwd_input_wait(k)
         with jax.named_scope('fwd_layers'):
-            lax.fori_loop(0, SEG, fwd_layer, k, unroll=UNROLL)
+            lax.fori_loop(0, SEG // GROUP, fwd_group, k)
 
         @pl.when(row < n_rows - 1)
         def _():
@@ -242,25 +246,34 @@
         mean_dot = jnp.mean(grad_hat * x_hat, axis=-1, keepdims=True)
         grad_x = inv_rms * (grad_hat - x_hat * mean_dot)
         grads[layer, k] = (grad_out.astype(F32) + grad_x).astype(BF16)
+
+    def bwd_group(group, k):
+        for step in range(GROUP):
+            bwd_layer(group * GROUP + step, k)
+
+        @pl.when((row > 0) & (group == SEG // GROUP - 1))
+        def _():
+            rcopy(grads.at[0, k], grads.at[SEG, k], bwd_send, bwd_recv.at[k], me - SEG).start()
+        for step in range(GROUP):
+            grad_ship(SEG - 1 - group * GROUP - step, k).start()
         return k
 
-    def bwd_output(k):
-        @pl.when(row > 0)
-        def _():
-            rcopy(grads.at[0, k], grads.at[SEG, k], bwd_send, bwd_recv.at[k], me - SEG).start()
-        for layer in range(SEG):
-            grad_ship(layer, k).start()
-
-    def both_layers(step, k):
-        fwd_layer(step, k)
-        bwd_layer(step, k - 1)
+    def both_group(group, k):
+        for step in range(GROUP):
+            fwd_layer(group * GROUP + step, k)
+            bwd_layer(group * GROUP + step, k - 1)
+
+        @pl.when((row > 0) & (group == SEG // GROUP - 1))
+        def _():
+            rcopy(grads.at[0, k - 1], grads.at[SEG, k - 1], bwd_send, bwd_recv.at[k - 1], me - SEG).start()
+        for step in range(GROUP):
+            grad_ship(SEG - 1 - group * GROUP - step, k - 1).start()
         return k
 
     def both_chunks(k, carry):
         fwd_input_wait(k)
         with jax.named_scope('both_layers'):
-            lax.fori_loop(0, SEG, both_layers, k, unroll=BOTH_UNROLL)
-        bwd_output(k - 1)
+            lax.fori_loop(0, SEG // GROUP, both_group, k)
         top_grad(k)
         for layer in range(SEG):
             act_ship(layer, k).start()
@@ -302,49 +315,15 @@
         with jax.named_scope('value_blocks'):
             lax.fori_loop(0, 2 * N_CHUNKS, value_block, 0)
 
-    @pl.when(row < n_rows - 1)
+    @pl.when(row < n_rows - LATE_ROWS)
     def _():
         value_phase()
-
-    def bwd_chunk(k, carry):
-        @pl.when(row < n_rows - 1)
-        def _():
-            with jax.named_scope('bwd_wait'):
-                rcopy(grads.at[SEG, k], grads.at[SEG, k], bwd_send, bwd_recv.at[k], me).wait_recv()
-
-        with jax.named_scope('bwd_layers'):
-            lax.fori_loop(0, SEG, bwd_layer, k, unroll=UNROLL)
-        bwd_output(k)
-        return carry
-
-    lax.fori_loop(jnp.where(row == n_rows - 1, N_CHUNKS - 1, 0), N_CHUNKS, bwd_chunk, 0)
-
-    def dg_ship(layer):
-        return rcopy(dg_part.at[layer], dg_stash.at[r], dg_send, dg_recv, row_base + layer)
-
-    for step in range(1, SEG):
-        dg_ship(lax.rem(r + step, SEG)).start()
-    dg_stash[r] = dg_part[r]
-
-    @pl.when(row == n_rows - 1)
-    def _():
-        rest = loss_stash.at[pl.ds(0, SEG - 1)]
-        rcopy(rest, rest, lrow_send, lrow_recv, me).wait_recv()
-        loss_total[...] = jnp.sum(loss_stash[...], axis=0)
-        for step in range(1, n_rows):
-            rcopy(loss_total, loss_total, lcol_send, lcol_recv, me - step * SEG).start()
-
-    @pl.when(row == n_rows - 1)
-    def _():
-        value_phase()
-
-    for k in range(N_CHUNKS):
-        grad_stash[k, r] = grads[r + 1, k]
 
     def weight_block(k, carry):
         rows = SEG * chunk
         with jax.named_scope('gs_wait'):
             rcopy(rest, rest, gs_send, gs_recv.at[k], me).wait_recv()
+        grad_stash[k, r] = grads[r + 1, k]
         normed = act_stash[k, pl.ds(0, SEG)].reshape(rows, d_model)
         grad_out = grad_stash[k, pl.ds(0, SEG)].reshape(rows, d_model)
         for part in range(0, d_ff, COLS):
@@ -355,8 +334,43 @@
             dwd_t[:, cols] += dot_tn(grad_out, value_stash[k, :, :, cols].reshape(rows, COLS))
         return carry
 
+    def bwd_chunk(k, carry):
+        @pl.when(row < n_rows - 1)
+        def _():
+            with jax.named_scope('bwd_wait'):
+                rcopy(grads.at[SEG, k], grads.at[SEG, k], bwd_send, bwd_recv.at[k], me).wait_recv()
+
+        with jax.named_scope('bwd_layers'):
+            lax.fori_loop(0, SEG // GROUP, bwd_group, k)
+
+        @pl.when((row < n_rows - LATE_ROWS) & (k > 0) & (k < N_CHUNKS - 1))
+        def _():
+            weight_block(k - 1, 0)
+        return carry
+
+    lax.fori_loop(jnp.where(row == n_rows - 1, N_CHUNKS - 1, 0), N_CHUNKS, bwd_chunk, 0)
+
+    def dg_ship(layer):
+        return rcopy(dg_part.at[layer], dg_stash.at[r], dg_send, dg_recv, row_base + layer)
+
+    for step in range(1, SEG):
+        dg_ship(lax.rem(r + step, SEG)).start()
+    dg_stash[r] = dg_part[r]
+
+    @pl.when(row >= n_rows - LATE_ROWS)
+    def _():
+        value_phase()
+
     with jax.named_scope('weight_blocks'):
-        lax.fori_loop(0, N_CHUNKS, weight_block, 0)
+        lax.fori_loop(jnp.where(row < n_rows - LATE_ROWS, N_CHUNKS - 2, 0), N_CHUNKS, weight_block, 0)
+    @pl.when(row == n_rows - 1)
+    def _():
+        rest_row = loss_stash.at[pl.ds(0, SEG - 1)]
+        rcopy(rest_row, rest_row, lrow_send, lrow_recv, me).wait_recv()
+        loss_total[...] = jnp.sum(loss_stash[...], axis=0)
+        for step in range(1, n_rows):
+            rcopy(loss_total, loss_total, lcol_send, lcol_recv, me - step * SEG).start()
+
     with jax.named_scope('turn'):
         dwd_ref[0] = dwd_t[...].T
 

time: 158 us -> 146 us (0.924)
  Pallas kernels: 152 us -> 140 us
    pallas_call x1, Pallas kernels: 152 us -> 140 us  [stage_body(): pl.pallas_call(functools.partial(step_kernel, n_stages, loss_scale), out_...]
where the time goes in v4:
time: 146 us
  Pallas kernels  140 us (96%)
  local copies, waits for them, and re-layouts  3.93 us (3%)
  between operations  2.41 us (2%)
    pallas_call x1, Pallas kernels, stage_body(): pl.pallas_call(functools.partial(step_kernel, n_stages, loss_scale), out_...  140 us
    unnamed x7, local copies, waits for them, and re-layouts  3.93 us

profile of v4, /device:TPU:97, one launch (start us, length us, event | category | flops | bytes accessed | tf_op | source)
XLA Modules:
  0.0 146.1 jit_solution(17374682633824346802)
XLA Ops:
  0.6 139.8 %shard_map.84 = (f32[1,256,1024]{2,1,0:T(8,128)}, f32[1,1024,256]{2,1,0:T(8,128)}, f32[1,256]{1,0:T(1,128)}, f32[1]{0:T(128)}) custom-call(bf16[4096,256]{1,0:T(8,128)(2,1)} %bitcast.2, bf16[4096,256]{1,0:T(8,128)(2,1)} %bitcast.3, bf16[1,256,1024]{2,1,0:T(8,128)(2,1)} %wu_hbm.1, bf16[1,1024,256]{2,1,0:T(8,128)(2,1)} %wd_hbm.1, f32[1,256]{1,0:T(1,128)} %gain_ref.1), custom_call_target="tpu_custom_call" | custom-call | tf_op jit(solution)/shard_map/pallas_call | solution.py:449
  140.4 0.0 copy-start
  140.4 0.0 copy-start.1
  140.4 2.4 %copy.13 = f32[1,256,1024]{2,1,0:T(8,128)} copy(f32[1,256,1024]{2,1,0:T(8,128)} %get-tuple-element.8) | data formatting | bytes 2097152
  142.8 0.0 copy-done
  142.8 1.0 copy.14
  143.8 0.0 copy-done.1
  143.8 0.6 copy.15
Async XLA Ops:
  140.4 2.4 %copy-start = (f32[1,1024,256]{2,1,0:T(8,128)S(1)}, f32[1,1024,256]{2,1,0:T(8,128)}, u32[]{:S(2)}) copy-start(f32[1,1024,256]{2,1,0:T(8,128)} %get-tuple-element.9) | copy-start | bytes 3145732
  140.4 3.4 %copy-start.1 = (f32[1,256]{1,0:T(1,128)S(1)}, f32[1,256]{1,0:T(1,128)}, u32[]{:S(2)}) copy-start(f32[1,256]{1,0:T(1,128)} %get-tuple-element.10) | copy-start | bytes 3076
